TPU v7x, 32 devices: a whole 2x2x4 slice. The times are simulated.
32 devices in a mesh: gx: 8 (over z, core), gy: 4 (over y, x).
Axes of the slice: x: 2, y: 2, z: 4, core: 2. Of those that a mesh axis runs over, the one named last changes fastest.
Arguments:
- density: float32 [256, 256, 256], P('gx', 'gy'), may hold values from 0.05 to 2
Outputs:
- potential: float32 [256, 256, 256], P('gx', 'gy')
- energy: float32 [], replicated
All inputs are finite; a program needn't handle non-finite values.
Results may differ from a plain program's by a relative error of at most 0.00005.
Values sent between devices are 32-bit elements.
A program may use at most 128 MiB of HBM per device.

v0:
```python
import functools
import math

import jax
import jax.numpy as jnp
import numpy as np
from jax import lax
from jax.experimental import pallas as pl
from jax.experimental.pallas import tpu as pltpu
from jax.sharding import PartitionSpec as P

spacing = 1.0
highest = lax.Precision.HIGHEST
pbe_kappa = 0.804
pbe_mu = 0.2195149727645171
pbe_beta = 0.06672455060314922
pbe_gamma = 0.031090690869654894
pw_coef = 0.0310907
pw_alpha = 0.2137
pw_first = 7.5957
pw_second = 3.5876
pw_third = 1.6382
pw_fourth = 0.49294


def xc_energy(electrons, grad_sq):
    third = jnp.exp(jnp.log(electrons) * (1.0 / 3.0))
    k_fermi = (3.0 * math.pi**2) ** (1.0 / 3.0) * third
    exch_unif = -0.75 / math.pi * k_fermi
    inv_sq = grad_sq / (4.0 * k_fermi * electrons * electrons)
    s_square = inv_sq / k_fermi
    enhance = 1.0 + pbe_kappa - pbe_kappa / (1.0 + (pbe_mu / pbe_kappa) * s_square)
    wigner = (3.0 / (4.0 * math.pi)) ** (1.0 / 3.0) / third
    root_rs = jnp.sqrt(wigner)
    series = (
        2.0
        * pw_coef
        * root_rs
        * (pw_first + root_rs * (pw_second + root_rs * (pw_third + root_rs * pw_fourth)))
    )
    corr_unif = -2.0 * pw_coef * (1.0 + pw_alpha * wigner) * jnp.log(1.0 + 1.0 / series)
    t_square = inv_sq * (math.pi / 4.0)
    factor = (pbe_beta / pbe_gamma) / (jnp.exp(corr_unif * (-1.0 / pbe_gamma)) - 1.0)
    scaled = factor * t_square
    gradient_term = pbe_gamma * jnp.log(
        1.0 + (pbe_beta / pbe_gamma) * t_square * (1.0 + scaled) / (1.0 + scaled + scaled * scaled)
    )
    return electrons * (exch_unif * enhance + corr_unif + gradient_term)


def deriv_matrix(count):
    positions = np.arange(count)
    signed = np.where(positions < count // 2, positions, positions - count)
    signed = np.where(positions == count // 2, 0, signed)
    waves = signed * (2.0 * math.pi / (count * spacing))
    phase = (positions[:, None] * positions[None, :] % count) * (2.0 * math.pi / count)
    cosine, sine = np.cos(phase), np.sin(phase)
    first = (cosine.T * waves[None, :]) @ sine
    second = (sine.T * waves[None, :]) @ cosine
    return ((first - second) / count).astype(np.float32)


def far_first(count):
    return sorted(range(1, count), key=lambda k: abs(2 * k - count))


def kernel(
    num_gx, num_gy, zc,
    n_hbm, dmx_hbm, dmy_hbm, dmz_hbm,
    out_ref, energy_ref,
    n_ref, dmx_ref, dmy_ref, dmz_ref,
    n_t, lx1, rx1, gx_t, gx, ly1, ry1, gy, gz, fx_t, lx2, rx2, dx_t, ly2, ry2, dy,
    acc, part_y, tot_y, part_x,
    xs_sem, xr_sem, ys_sem, yr_sem, es_sem, er_sem, in_sem,
):
    rows_x, rows_y, count_z = n_ref.shape
    block_y = rows_y // num_gx
    block_x = rows_x // num_gy
    count_x = rows_x * num_gx
    count_y = rows_y * num_gy
    chunks = count_z // zc
    me_x = lax.axis_index("gx")
    me_y = lax.axis_index("gy")

    def peer_x(k):
        return lax.rem(me_x + k, num_gx)

    def peer_y(k):
        return lax.rem(me_y + k, num_gy)

    def zs(c):
        return pl.ds(c * zc, zc)

    def x_block(i):
        return pl.ds(i * block_y, block_y)

    def x_rows(i):
        return pl.ds(pl.multiple_of(i * rows_x, rows_x), rows_x)

    def y_block(i):
        return pl.ds(i * block_x, block_x)

    def y_rows(i):
        return pl.ds(pl.multiple_of(i * rows_y, rows_y), rows_y)

    loads = [
        pltpu.make_async_copy(n_hbm.at[:, :, zs(c)], n_ref.at[:, :, zs(c)], in_sem.at[c])
        for c in range(chunks)
    ]
    pairs = ((dmz_hbm, dmz_ref), (dmy_hbm, dmy_ref), (dmx_hbm, dmx_ref))
    tables = [
        pltpu.make_async_copy(source, target, in_sem.at[chunks + place])
        for place, (source, target) in enumerate(pairs)
    ]
    for copy in loads + tables:
        copy.start()
    barrier = pltpu.get_barrier_semaphore()
    for k in range(1, num_gx):
        pl.semaphore_signal(
            barrier, inc=1, device_id={"gx": peer_x(k)}, device_id_type=pl.DeviceIdType.MESH
        )
    for k in range(1, num_gy):
        pl.semaphore_signal(
            barrier, inc=1, device_id={"gy": peer_y(k)}, device_id_type=pl.DeviceIdType.MESH
        )
    def send_x(phase, c, source, target, forward):
        copies = []
        for k in far_first(num_gx):
            to = peer_x(k)
            if forward:
                src, dst = source.at[x_block(to), :, zs(c)], target.at[:, x_rows(me_x), zs(c)]
            else:
                src, dst = source.at[:, x_rows(to), zs(c)], target.at[x_block(me_x), :, zs(c)]
            copy = pltpu.make_async_remote_copy(
                src_ref=src, dst_ref=dst,
                send_sem=xs_sem.at[phase, c, k], recv_sem=xr_sem.at[phase, c, k],
                device_id={"gx": to}, device_id_type=pl.DeviceIdType.MESH,
            )
            copy.start()
            copies.append(copy)
        if forward:
            target[:, x_rows(me_x), zs(c)] = source[x_block(me_x), :, zs(c)]
        else:
            target[x_block(me_x), :, zs(c)] = source[:, x_rows(me_x), zs(c)]
        return copies

    def send_y(phase, c, source, target, forward):
        copies = []
        for k in far_first(num_gy):
            to = peer_y(k)
            if forward:
                src, dst = source.at[y_block(to), :, zs(c)], target.at[:, y_rows(me_y), zs(c)]
            else:
                src, dst = source.at[:, y_rows(to), zs(c)], target.at[y_block(me_y), :, zs(c)]
            copy = pltpu.make_async_remote_copy(
                src_ref=src, dst_ref=dst,
                send_sem=ys_sem.at[phase, c, k], recv_sem=yr_sem.at[phase, c, k],
                device_id={"gy": to}, device_id_type=pl.DeviceIdType.MESH,
            )
            copy.start()
            copies.append(copy)
        if forward:
            target[:, y_rows(me_y), zs(c)] = source[y_block(me_y), :, zs(c)]
        else:
            target[y_block(me_y), :, zs(c)] = source[:, y_rows(me_y), zs(c)]
        return copies

    def arrived(copies):
        for copy in copies:
            copy.wait_recv()

    def lines(matrix, source, target, c):
        @pl.loop(0, source.shape[0])
        def _(i):
            target[i, :, zs(c)] = jnp.dot(
                matrix[...], source[i, :, zs(c)],
                precision=highest, preferred_element_type=jnp.float32,
            )

    step = min(8, rows_y)

    def turn_in(source, target, c):
        @pl.loop(0, rows_y // step)
        def _(j):
            y0 = pl.multiple_of(j * step, step)
            target[pl.ds(y0, step), :, zs(c)] = jnp.swapaxes(
                source[:, pl.ds(y0, step), zs(c)], 0, 1
            )

    def turn_out(source, target, c):
        @pl.loop(0, rows_y // step)
        def _(j):
            y0 = pl.multiple_of(j * step, step)
            target[:, pl.ds(y0, step), zs(c)] = jnp.swapaxes(
                source[pl.ds(y0, step), :, zs(c)], 0, 1
            )

    group = min(rows_x, max(1, 256 // rows_y))

    def along_z(source):
        def at(i):
            return pl.ds(i * group, group)

        def product(i):
            flat = source[at(i)].reshape(group * rows_y, count_z)
            result = jnp.dot(
                flat, dmz_ref[...], precision=highest, preferred_element_type=jnp.float32
            )
            return result.reshape(group, rows_y, count_z)

        return at, product

    sent = []
    every = range(chunks)
    fy1, fx1 = [], []
    for c in every:
        loads[c].wait()
        turn_in(n_ref, n_t, c)
        if c == 0:
            pl.semaphore_wait(barrier, num_gx + num_gy - 2)
        fx1.append(send_x(0, c, n_t, lx1, True))
        fy1.append(send_y(0, c, n_ref, ly1, True))
    for copy in tables:
        copy.wait()
    at, product = along_z(n_ref)

    @pl.loop(0, rows_x // group)
    def _(i):
        gz[at(i)] = product(i)

    by1, bx1 = [], []
    for c in every:
        arrived(fy1[c])
        lines(dmy_ref, ly1, ry1, c)
        by1.append(send_y(1, c, ry1, gy, False))
    for c in every:
        arrived(fx1[c])
        lines(dmx_ref, lx1, rx1, c)
        bx1.append(send_x(1, c, rx1, gx_t, False))

    acc[...] = jnp.zeros_like(acc)
    part = min(rows_y, 32)
    fx2, fy2 = [], []
    for c in every:
        arrived(by1[c])
        arrived(bx1[c])
        turn_out(gx_t, gx, c)

        @pl.loop(0, rows_x)
        def _(i):
            @pl.loop(0, rows_y // part)
            def _(j):
                where = (i, pl.ds(pl.multiple_of(j * part, part), part), zs(c))
                dens, grad_x, grad_y, grad_z = n_ref[where], gx[where], gy[where], gz[where]
                grad_sq = grad_x * grad_x + grad_y * grad_y + grad_z * grad_z
                value, pull = jax.vjp(xc_energy, dens, grad_sq)
                d_dens, d_grad = pull(jnp.ones_like(value))
                twice = 2.0 * d_grad
                out_ref[where] = d_dens
                gx[where] = twice * grad_x
                gy[where] = twice * grad_y
                gz[where] = twice * grad_z
                acc[...] += value

        turn_in(gx, fx_t, c)
        fx2.append(send_x(2, c, fx_t, lx2, True))
        fy2.append(send_y(2, c, gy, ly2, True))

    energy = jnp.sum(acc[...].reshape(-1, 8, zc), axis=0)
    part_y[me_y] = energy
    energy_copies = []
    for k in range(1, num_gy):
        copy = pltpu.make_async_remote_copy(
            src_ref=part_y.at[me_y], dst_ref=part_y.at[me_y],
            send_sem=es_sem.at[0, k], recv_sem=er_sem.at[0, k],
            device_id={"gy": peer_y(k)}, device_id_type=pl.DeviceIdType.MESH,
        )
        copy.start()
        energy_copies.append(copy)

    at, product = along_z(gz)

    @pl.loop(0, rows_x // group)
    def _(i):
        out_ref[at(i)] = out_ref[at(i)] - product(i)

    arrived(energy_copies)
    sent.append(energy_copies)
    tot_y[...] = jnp.sum(part_y[...], axis=0)
    part_x[me_x] = tot_y[...]
    energy_copies = []
    for k in range(1, num_gx):
        copy = pltpu.make_async_remote_copy(
            src_ref=tot_y, dst_ref=part_x.at[me_x],
            send_sem=es_sem.at[1, k], recv_sem=er_sem.at[1, k],
            device_id={"gx": peer_x(k)}, device_id_type=pl.DeviceIdType.MESH,
        )
        copy.start()
        energy_copies.append(copy)

    bx2, by2 = [], []
    for c in every:
        arrived(fy2[c])
        lines(dmy_ref, ly2, ry2, c)
        by2.append(send_y(3, c, ry2, dy, False))
        arrived(fx2[c])
        lines(dmx_ref, lx2, rx2, c)
        bx2.append(send_x(3, c, rx2, dx_t, False))

    arrived(energy_copies)
    sent.append(energy_copies)
    cells = float(count_x * count_y * count_z)
    total = jnp.sum(part_x[...], axis=0)
    energy_ref[...] = jnp.sum(total, axis=(0, 1), keepdims=True) * (1.0 / cells)

    for c in every:
        arrived(by2[c])
        arrived(bx2[c])

        @pl.loop(0, rows_y // step)
        def _(j):
            y0 = pl.multiple_of(j * step, step)
            where = (slice(None), pl.ds(y0, step), zs(c))
            turned = jnp.swapaxes(dx_t[pl.ds(y0, step), :, zs(c)], 0, 1)
            out_ref[where] = out_ref[where] - (dy[where] + turned)

    for copies in sent + fx1 + fy1 + bx1 + by1 + fx2 + fy2 + bx2 + by2:
        for copy in copies:
            copy.wait_send()


def body(num_gx, num_gy, density):
    rows_x, rows_y, count_z = density.shape
    count_x = rows_x * num_gx
    count_y = rows_y * num_gy
    zc = 128 if count_z % 128 == 0 else count_z
    chunks = count_z // zc
    block_y = rows_y // num_gx
    block_x = rows_x // num_gy
    straight = (rows_x, rows_y, count_z)
    turned = (rows_y, rows_x, count_z)
    lines_x = (block_y, count_x, count_z)
    lines_y = (block_x, count_y, count_z)
    shapes = [
        straight, (count_x, count_x), (count_y, count_y), (count_z, count_z),
        turned, lines_x, lines_x, turned, straight,
        lines_y, lines_y, straight, straight,
        turned, lines_x, lines_x, turned,
        lines_y, lines_y, straight,
        (min(rows_y, 32), zc), (num_gy, 8, zc), (8, zc), (num_gx, 8, zc),
    ]
    vmem = pl.BlockSpec(memory_space=pltpu.VMEM)
    potential, partial = pl.pallas_call(
        functools.partial(kernel, num_gx, num_gy, zc),
        out_shape=(
            pltpu.VMEM(straight, jnp.float32),
            jax.ShapeDtypeStruct((1, 1), jnp.float32),
        ),
        in_specs=[pl.BlockSpec(memory_space=pltpu.HBM)] * 4,
        out_specs=(vmem, vmem),
        scratch_shapes=[pltpu.VMEM(shape, jnp.float32) for shape in shapes]
        + [
            pltpu.SemaphoreType.DMA((4, chunks, num_gx)),
            pltpu.SemaphoreType.DMA((4, chunks, num_gx)),
            pltpu.SemaphoreType.DMA((4, chunks, num_gy)),
            pltpu.SemaphoreType.DMA((4, chunks, num_gy)),
            pltpu.SemaphoreType.DMA((2, num_gx)),
            pltpu.SemaphoreType.DMA((2, num_gx)),
            pltpu.SemaphoreType.DMA((chunks + 3,)),
        ],
        compiler_params=pltpu.CompilerParams(
            collective_id=0, has_side_effects=True, vmem_limit_bytes=67043328 - 4 * density.size - 2**16
        ),
    )(
        density,
        jnp.asarray(deriv_matrix(count_x)),
        jnp.asarray(deriv_matrix(count_y)),
        jnp.asarray(deriv_matrix(count_z).T.copy()),
    )
    return (potential, partial.reshape(()))


def solution(mesh):
    in_specs = (P("gx", "gy", None),)
    out_specs = (P("gx", "gy", None), P())
    run = functools.partial(body, mesh.shape["gx"], mesh.shape["gy"])
    return jax.shard_map(run, mesh=mesh, in_specs=in_specs, out_specs=out_specs, check_vma=False)
```

profile of v0, /device:TPU:9, one launch (start us, length us, event | category | flops | bytes accessed | tf_op | source)
XLA Modules:
  0.0 192.0 jit_solution(4591625897726223931)
XLA Ops:
  0.6 188.3 %shard_map.59 = (f32[32,64,256]{2,1,0:T(8,128)S(1)}, f32[1,1]{1,0:T(1,128)}) custom-call(f32[32,64,256]{2,1,0:T(8,128)} %n_hbm.1, f32[256,256]{1,0:T(8,128)} %constant.4.clone.dmx_hbm.dmy_hbm, f32[256,256]{1,0:T(8,128)} %constant.4.clone.dmx_hbm.dmy_hbm, f32[256,256]{1,0:T(8,128)} %constant.5.clone.dmz_hbm), custom_call_target="tpu_custom_call" | custom-call | tf_op jit(solution)/shard_map/pallas_call | solution.py:353
  189.0 1.3 copy.8
where the time goes:
time: 192 us
  Pallas kernels  188 us (98%)
  between operations  2.33 us (1%)
    pallas_call x1, Pallas kernels, body(): pl.pallas_call(functools.partial(kernel, num_gx, num_gy, zc), out_shape=(...  188 us

commit v1 on v0

--- a/solution.py
+++ b/solution.py
@@ -327,6 +327,590 @@
     for copies in sent + fx1 + fy1 + bx1 + by1 + fx2 + fy2 + bx2 + by2:
         for copy in copies:
             copy.wait_send()
+
+
+def chip_kernel(
+    num_gx, num_gy, parts,
+    n_hbm, dmx_hbm, dmy_hbm, dmz_hbm,
+    out_ref, energy_ref,
+    n_ref, dmx_ref, dmy_ref, dmz_ref,
+    n_t, n_lines, g_lines, gx_t, gx, fx_t, f_lines, dx_t,
+    ly1, ly2, ry, gy, dy, gz,
+    far_n, far_ly, far_ry, far_gy, far_other, far_gz,
+    acc, part_y, tot_y, part_x,
+    ns_sem, nr_sem, gs_sem, gr_sem, fs_sem, fr_sem, ds_sem, dr_sem,
+    ys_sem, yr_sem, ws_sem, wr_sem, os_sem, or_sem, es_sem, er_sem, in_sem,
+):
+    rows_x, rows_y, count_z = n_ref.shape
+    half = count_z // 2
+    chip_x = 2 * rows_x
+    block_x = rows_x // num_gy
+    far_block = chip_x // num_gy
+    count_x = rows_x * num_gx
+    count_y = rows_y * num_gy
+    span = rows_y // parts
+    me_x = lax.axis_index("gx")
+    me_y = lax.axis_index("gy")
+    core = lax.rem(me_x, 2)
+    chip = me_x // 2
+    chips = num_gx // 2
+    is_inner = jnp.logical_and(chip > 0, chip < chips - 1)
+    low = chip < 2
+    inner = jnp.where(low, 1, 2)
+    outer = jnp.where(low, 0, 3)
+    opposite = 3 - inner
+    far_outer = 3 - outer
+    mate = chip * 2 + (1 - core)
+    every = range(parts)
+    lanes_count = 2
+
+    def zs(c):
+        if isinstance(c, int):
+            return pl.ds(c * half, half)
+        return pl.ds(pl.multiple_of(c * half, half), half)
+
+    def ys(s):
+        return pl.ds(s * span, span)
+
+    def x_rows(device):
+        return pl.ds(pl.multiple_of(device * rows_x, rows_x), rows_x)
+
+    def chip_rows(which):
+        return pl.ds(pl.multiple_of(which * chip_x, chip_x), chip_x)
+
+    def local_rows(start, size):
+        return pl.ds(pl.multiple_of(start, rows_x), size)
+
+    def peer_y(k):
+        return lax.rem(me_y + k, num_gy)
+
+    def y_rows(i):
+        return pl.ds(pl.multiple_of(i * rows_y, rows_y), rows_y)
+
+    def to_x(device, source, target, send, recv):
+        return pltpu.make_async_remote_copy(
+            src_ref=source, dst_ref=target, send_sem=send, recv_sem=recv,
+            device_id={"gx": device}, device_id_type=pl.DeviceIdType.MESH,
+        )
+
+    def landed(target, recv):
+        to_x(mate, target, target, recv, recv).wait_recv()
+
+    loads = [
+        pltpu.make_async_copy(n_hbm.at[:, :, zs(c)], n_ref.at[:, :, zs(c)], in_sem.at[c])
+        for c in range(lanes_count)
+    ]
+    pairs = ((dmz_hbm, dmz_ref), (dmy_hbm, dmy_ref), (dmx_hbm, dmx_ref))
+    tables = [
+        pltpu.make_async_copy(source, target, in_sem.at[lanes_count + place])
+        for place, (source, target) in enumerate(pairs)
+    ]
+    for copy in loads + tables:
+        copy.start()
+    barrier = pltpu.get_barrier_semaphore()
+    for k in range(1, num_gx):
+        pl.semaphore_signal(
+            barrier, inc=1, device_id={"gx": lax.rem(me_x + k, num_gx)},
+            device_id_type=pl.DeviceIdType.MESH,
+        )
+    for k in range(1, num_gy):
+        pl.semaphore_signal(
+            barrier, inc=1, device_id={"gy": peer_y(k)}, device_id_type=pl.DeviceIdType.MESH
+        )
+
+    def y_copies(phase, c, source, target, forward):
+        copies = []
+        for k in far_first(num_gy):
+            to = peer_y(k)
+            theirs, mine = pl.ds(to * block_x, block_x), pl.ds(me_y * block_x, block_x)
+            if forward:
+                src, dst = source.at[theirs, :, zs(c)], target.at[:, y_rows(me_y), zs(c)]
+            else:
+                src, dst = source.at[:, y_rows(to), zs(c)], target.at[mine, :, zs(c)]
+            copies.append(pltpu.make_async_remote_copy(
+                src_ref=src, dst_ref=dst,
+                send_sem=ys_sem.at[phase, c, k], recv_sem=yr_sem.at[phase, c, k],
+                device_id={"gy": to}, device_id_type=pl.DeviceIdType.MESH,
+            ))
+        return copies
+
+    y_plan = ((n_ref, ly1, True), (ry, gy, False), (gy, ly2, True), (ry, dy, False))
+
+    def y_send(phase, c):
+        source, target, forward = y_plan[phase]
+        for copy in y_copies(phase, c, source, target, forward):
+            copy.start()
+        mine = pl.ds(me_y * block_x, block_x)
+        if forward:
+            target[:, y_rows(me_y), zs(c)] = source[mine, :, zs(c)]
+        else:
+            target[mine, :, zs(c)] = source[:, y_rows(me_y), zs(c)]
+
+    def y_wait(phase, c, sent):
+        for copy in y_copies(phase, c, *y_plan[phase]):
+            if sent:
+                copy.wait_send()
+            else:
+                copy.wait_recv()
+
+    def far_copies(phase):
+        copies = []
+        for k in far_first(num_gy):
+            to = peer_y(k)
+            if phase == 0:
+                src = far_n.at[pl.ds(to * far_block, far_block)]
+                dst = far_ly.at[:, y_rows(me_y), :]
+            else:
+                src = far_ry.at[:, y_rows(to), :]
+                dst = far_gy.at[pl.ds(me_y * far_block, far_block)]
+            copies.append(pltpu.make_async_remote_copy(
+                src_ref=src, dst_ref=dst,
+                send_sem=ws_sem.at[phase, k], recv_sem=wr_sem.at[phase, k],
+                device_id={"gy": to}, device_id_type=pl.DeviceIdType.MESH,
+            ))
+        return copies
+
+    def far_send(phase):
+        for copy in far_copies(phase):
+            copy.start()
+        mine = pl.ds(me_y * far_block, far_block)
+        if phase == 0:
+            far_ly[:, y_rows(me_y), :] = far_n[mine]
+        else:
+            far_gy[mine] = far_ry[:, y_rows(me_y), :]
+
+    def far_wait(phase, sent):
+        for copy in far_copies(phase):
+            if sent:
+                copy.wait_send()
+            else:
+                copy.wait_recv()
+
+    def product(left, right):
+        return jnp.dot(left, right, precision=highest, preferred_element_type=jnp.float32)
+
+    def y_lines(source, c):
+        @pl.loop(0, block_x)
+        def _(i):
+            ry[i, :, zs(c)] = product(dmy_ref[...], source[i, :, zs(c)])
+
+    group = min(rows_x, max(1, 256 // rows_y))
+
+    def along_z(source, i):
+        flat = source[pl.ds(i * group, group)].reshape(group * rows_y, count_z)
+        return product(flat, dmz_ref[...]).reshape(group, rows_y, count_z)
+
+    step = min(8, span)
+
+    def turned(source, target, s):
+        @pl.loop(0, span // step)
+        def _(j):
+            y0 = pl.multiple_of(s * span + j * step, step)
+            target[pl.ds(y0, step)] = jnp.swapaxes(source[:, pl.ds(y0, step), :], 0, 1)
+
+    def n_sends(s, role):
+        copies = []
+        if role == "outer":
+            for j in range(2):
+                copies.append(to_x(
+                    inner * 2 + j, n_t.at[ys(s), :, zs(j)], n_lines.at[ys(s), x_rows(me_x), :],
+                    ns_sem.at[j, s], nr_sem.at[core, s],
+                ))
+        else:
+            for j in range(2):
+                copies.append(to_x(
+                    opposite * 2 + j, n_t.at[ys(s), :, zs(j)], n_lines.at[ys(s), x_rows(me_x), :],
+                    ns_sem.at[j, s], nr_sem.at[2 + core, s],
+                ))
+            copies.append(to_x(
+                mate, n_t.at[ys(s), :, zs(1 - core)], n_lines.at[ys(s), x_rows(me_x), :],
+                ns_sem.at[2, s], nr_sem.at[4, s],
+            ))
+        return copies
+
+    def forward_copy(lines, send, recv, s):
+        part = lines.at[ys(s), chip_rows(outer), :]
+        return to_x(opposite * 2 + core, part, part, send.at[3, s], recv.at[5, s])
+
+    def from_outer(lines, recv, s):
+        for j in range(2):
+            landed(lines.at[ys(s), x_rows(outer * 2 + j), :], recv.at[j, s])
+
+    def f_sends(s, role):
+        copies = []
+        if role == "outer":
+            for j in range(2):
+                copies.append(to_x(
+                    inner * 2 + j, fx_t.at[ys(s), :, zs(j)], f_lines.at[ys(s), x_rows(me_x), :],
+                    fs_sem.at[j, s], fr_sem.at[core, s],
+                ))
+        else:
+            copies.append(to_x(
+                mate, fx_t.at[ys(s), :, zs(1 - core)], f_lines.at[ys(s), x_rows(me_x), :],
+                fs_sem.at[2, s], fr_sem.at[4, s],
+            ))
+        return copies
+
+    def back_copies(own, other, target, send, recv, s):
+        copies = []
+        for j in range(2):
+            copies.append(to_x(
+                outer * 2 + j, g_lines.at[ys(s), local_rows(other + j * rows_x, rows_x), :],
+                target.at[ys(s), :, zs(core)], send.at[j, s], recv.at[core, s],
+            ))
+        copies.append(to_x(
+            mate, g_lines.at[ys(s), local_rows(own + (1 - core) * rows_x, rows_x), :],
+            target.at[ys(s), :, zs(core)], send.at[2, s], recv.at[core, s],
+        ))
+        return copies
+
+    first_own, first_other, first_far = chip_x, jnp.where(low, 0, 2 * chip_x), jnp.where(low, 2 * chip_x, 0)
+    second_own, second_other = jnp.where(low, chip_x, 0), jnp.where(low, 0, chip_x)
+
+    def x_back(own, other, target, send, recv, s):
+        for copy in back_copies(own, other, target, send, recv, s):
+            copy.start()
+        target[ys(s), :, zs(core)] = g_lines[ys(s), local_rows(own + core * rows_x, rows_x), :]
+
+    def x_lines(source, first_row, rows, s):
+        @pl.loop(0, span)
+        def _(j):
+            y = s * span + j
+            matrix = dmx_ref[pl.ds(pl.multiple_of(first_row, chip_x), rows), :]
+            g_lines[y, pl.ds(0, rows), :] = product(matrix, source[y])
+
+    deep = min(rows_x, max(1, 32 // (span * lanes_count)))
+
+    def pointwise(s):
+        @pl.loop(0, span // step)
+        def _(j):
+            y0 = pl.multiple_of(s * span + j * step, step)
+            gx[:, pl.ds(y0, step), :] = jnp.swapaxes(gx_t[pl.ds(y0, step)], 0, 1)
+
+        @pl.loop(0, rows_x // deep)
+        def _(i):
+            where = (pl.ds(i * deep, deep), ys(s))
+            dens, grad_x, grad_y, grad_z = n_ref[where], gx[where], gy[where], gz[where]
+            grad_sq = grad_x * grad_x + grad_y * grad_y + grad_z * grad_z
+            value, pull = jax.vjp(xc_energy, dens, grad_sq)
+            d_dens, d_grad = pull(jnp.ones_like(value))
+            twice = 2.0 * d_grad
+            out_ref[where] = d_dens
+            gx[where] = twice * grad_x
+            gy[where] = twice * grad_y
+            gz[where] = twice * grad_z
+            acc[...] += value
+
+        turned(gx, fx_t, s)
+
+    def z_gradient():
+        @pl.loop(0, rows_x // group)
+        def _(i):
+            gz[pl.ds(i * group, group)] = along_z(n_ref, i)
+
+    def z_divergence():
+        @pl.loop(0, rows_x // group)
+        def _(i):
+            at = pl.ds(i * group, group)
+            out_ref[at] = out_ref[at] - along_z(gz, i)
+
+    def energy_copies(phase):
+        copies = []
+        count = num_gy if phase == 0 else num_gx
+        for k in range(1, count):
+            if phase == 0:
+                to, src, dst = {"gy": peer_y(k)}, part_y.at[me_y], part_y.at[me_y]
+            else:
+                to, src, dst = {"gx": lax.rem(me_x + k, num_gx)}, tot_y, part_x.at[me_x]
+            copies.append(pltpu.make_async_remote_copy(
+                src_ref=src, dst_ref=dst,
+                send_sem=es_sem.at[phase, k], recv_sem=er_sem.at[phase, k],
+                device_id=to, device_id_type=pl.DeviceIdType.MESH,
+            ))
+        return copies
+
+    def energy_first():
+        total = jnp.sum(acc[...].reshape(-1, 8, count_z), axis=0)
+        part_y[me_y] = total[:, :half] + total[:, half:]
+        for copy in energy_copies(0):
+            copy.start()
+
+    def energy_second():
+        for copy in energy_copies(0):
+            copy.wait_recv()
+        tot_y[...] = jnp.sum(part_y[...], axis=0)
+        part_x[me_x] = tot_y[...]
+        for copy in energy_copies(1):
+            copy.start()
+
+    def energy_last():
+        for copy in energy_copies(1):
+            copy.wait_recv()
+        cells = float(count_x * count_y * count_z)
+        total = jnp.sum(part_x[...], axis=0)
+        energy_ref[...] = jnp.sum(total, axis=(0, 1), keepdims=True) * (1.0 / cells)
+
+    def finish(s, sources):
+        for j in sources:
+            landed(dx_t.at[ys(s), :, zs(j)], dr_sem.at[j, s])
+
+        @pl.loop(0, span // step)
+        def _(j):
+            y0 = pl.multiple_of(s * span + j * step, step)
+            where = (slice(None), pl.ds(y0, step))
+            side = jnp.swapaxes(dx_t[pl.ds(y0, step)], 0, 1)
+            out_ref[where] = out_ref[where] - (dy[where] + side)
+
+    def start_n(role):
+        for s in every:
+            turned(n_ref, n_t, s)
+            for copy in n_sends(s, role):
+                copy.start()
+            if role == "inner":
+                n_lines[ys(s), x_rows(me_x), :] = n_t[ys(s), :, zs(core)]
+
+    def y_first(c):
+        y_wait(0, c, False)
+        y_lines(ly1, c)
+        y_send(1, c)
+
+    def y_second(c):
+        y_wait(2, c, False)
+        if c == 0:
+            for other in range(lanes_count):
+                y_wait(1, other, True)
+        y_lines(ly2, c)
+        y_send(3, c)
+
+    acc[...] = jnp.zeros_like(acc)
+    for c in range(lanes_count):
+        loads[c].wait()
+        if c == 0:
+            pl.semaphore_wait(barrier, num_gx + num_gy - 2)
+        y_send(0, c)
+
+    def outer_program():
+        start_n("outer")
+        for copy in tables:
+            copy.wait()
+        z_gradient()
+        for c in range(lanes_count):
+            y_first(c)
+        for c in range(lanes_count):
+            y_wait(1, c, False)
+        for s in every:
+            for j in range(2):
+                landed(gx_t.at[ys(s), :, zs(j)], gr_sem.at[j, s])
+            pointwise(s)
+            for copy in f_sends(s, "outer"):
+                copy.start()
+        for c in range(lanes_count):
+            y_send(2, c)
+        energy_first()
+        z_divergence()
+        energy_second()
+        for c in range(lanes_count):
+            y_second(c)
+        energy_last()
+        for c in range(lanes_count):
+            y_wait(3, c, False)
+        for s in every:
+            finish(s, (0, 1))
+        for s in every:
+            for copy in n_sends(s, "outer") + f_sends(s, "outer"):
+                copy.wait_send()
+
+    def inner_program():
+        start_n("inner")
+        for copy in tables:
+            copy.wait()
+        z_gradient()
+
+        def pass_on(lines, send, recv, s):
+            from_outer(lines, recv, s)
+            forward_copy(lines, send, recv, s).start()
+
+        y_first(0)
+        early = parts // 4
+        for s in range(early):
+            pass_on(n_lines, ns_sem, nr_sem, s)
+        y_first(1)
+        for s in range(early, parts):
+            pass_on(n_lines, ns_sem, nr_sem, s)
+
+        far_rows = chip_rows(opposite)
+        for s in every:
+            for j in range(2):
+                landed(n_lines.at[ys(s), x_rows(opposite * 2 + j), :], nr_sem.at[2 + j, s])
+        swap = to_x(mate, n_lines.at[:, far_rows, :], far_other, os_sem.at[0], or_sem.at[0])
+        swap.start()
+
+        @pl.loop(0, rows_y // 8)
+        def _(j):
+            y0 = pl.multiple_of(j * 8, 8)
+            far_n[:, pl.ds(y0, 8), :] = jnp.swapaxes(n_lines[pl.ds(y0, 8), far_rows, :], 0, 1)
+
+        far_send(0)
+        swap.wait_recv()
+        far_group = min(rows_y, max(1, 256 // chip_x))
+
+        @pl.loop(0, rows_y // far_group)
+        def _(i):
+            at = pl.ds(i * far_group, far_group)
+            here = n_lines[at, far_rows, :].reshape(far_group * chip_x, half)
+            there = far_other[at].reshape(far_group * chip_x, half)
+            result = product(here, dmz_ref[zs(core), zs(core)])
+            result = result + product(there, dmz_ref[zs(1 - core), zs(core)])
+            far_gz[at] = result.reshape(far_group, chip_x, half)
+
+        def far_lines():
+            far_wait(0, False)
+
+            @pl.loop(0, far_block)
+            def _(i):
+                far_ry[i] = product(dmy_ref[...], far_ly[i])
+
+            far_send(1)
+
+        def far_pointwise(s):
+            @pl.loop(0, span // step)
+            def _(j):
+                y0 = pl.multiple_of(s * span + j * step, step)
+                far_other[pl.ds(y0, step)] = jnp.swapaxes(far_gy[:, pl.ds(y0, step), :], 0, 1)
+
+            tall = min(32, chip_x)
+
+            @pl.loop(0, span)
+            def _(j):
+                y = s * span + j
+
+                @pl.loop(0, chip_x // tall)
+                def _(i):
+                    x0 = pl.multiple_of(i * tall, tall)
+                    near = pl.ds(x0, tall)
+                    line = pl.ds(pl.multiple_of(opposite * chip_x + x0, tall), tall)
+                    dens = n_lines[y, line, :]
+                    grad_x = g_lines[y, pl.ds(pl.multiple_of(first_far + x0, tall), tall), :]
+                    grad_y, grad_z = far_other[y, near, :], far_gz[y, near, :]
+                    grad_sq = grad_x * grad_x + grad_y * grad_y + grad_z * grad_z
+                    value, pull = jax.vjp(functools.partial(xc_energy, dens), grad_sq)
+                    (d_grad,) = pull(jnp.ones_like(value))
+                    f_lines[y, line, :] = 2.0 * d_grad * grad_x
+
+        for c in range(lanes_count):
+            y_wait(1, c, False)
+        lag = parts // 2
+        for s in every:
+            landed(n_lines.at[ys(s), chip_rows(far_outer), :], nr_sem.at[5, s])
+            landed(n_lines.at[ys(s), x_rows(mate), :], nr_sem.at[4, s])
+            x_lines(n_lines, (inner - 1) * chip_x, 3 * chip_x, s)
+            x_back(first_own, first_other, gx_t, gs_sem, gr_sem, s)
+            landed(gx_t.at[ys(s), :, zs(1 - core)], gr_sem.at[1 - core, s])
+            pointwise(s)
+            for copy in f_sends(s, "inner"):
+                copy.start()
+            f_lines[ys(s), x_rows(me_x), :] = fx_t[ys(s), :, zs(core)]
+            if s == lag:
+                far_lines()
+            if s >= lag:
+                pass_on(f_lines, fs_sem, fr_sem, s - lag)
+        for c in range(lanes_count):
+            y_send(2, c)
+        energy_first()
+        swap.wait_send()
+        far_wait(1, False)
+        for s in every:
+            far_pointwise(s)
+            if s < parts - lag:
+                pass_on(f_lines, fs_sem, fr_sem, lag + s)
+            for copy in back_copies(first_own, first_other, gx_t, gs_sem, gr_sem, s):
+                copy.wait_send()
+            landed(f_lines.at[ys(s), x_rows(mate), :], fr_sem.at[4, s])
+            landed(f_lines.at[ys(s), chip_rows(far_outer), :], fr_sem.at[5, s])
+            x_lines(f_lines, (inner - 1) * 2 * chip_x, 2 * chip_x, s)
+            x_back(second_own, second_other, dx_t, ds_sem, dr_sem, s)
+            if s == parts // 4:
+                y_second(0)
+            if s == parts // 2:
+                y_second(1)
+            if s == parts // 2 + 1:
+                energy_second()
+        z_divergence()
+        energy_last()
+        for c in range(lanes_count):
+            y_wait(3, c, False)
+        for s in every:
+            finish(s, (1 - core,))
+        for s in every:
+            for copy in n_sends(s, "inner") + f_sends(s, "inner"):
+                copy.wait_send()
+            forward_copy(n_lines, ns_sem, nr_sem, s).wait_send()
+            forward_copy(f_lines, fs_sem, fr_sem, s).wait_send()
+            for copy in back_copies(second_own, second_other, dx_t, ds_sem, dr_sem, s):
+                copy.wait_send()
+        for phase in range(2):
+            far_wait(phase, True)
+
+    pl.when(is_inner)(inner_program)
+    pl.when(jnp.logical_not(is_inner))(outer_program)
+
+    for c in range(lanes_count):
+        for phase in (0, 2, 3):
+            y_wait(phase, c, True)
+    for phase in range(2):
+        for copy in energy_copies(phase):
+            copy.wait_send()
+
+
+def chip_body(num_gx, num_gy, density):
+    rows_x, rows_y, count_z = density.shape
+    count_x = rows_x * num_gx
+    count_y = rows_y * num_gy
+    half = count_z // 2
+    parts = rows_y // 8
+    span = rows_y // parts
+    block_x = rows_x // num_gy
+    chip_x = 2 * rows_x
+    far_block = chip_x // num_gy
+    straight = (rows_x, rows_y, count_z)
+    turned = (rows_y, rows_x, count_z)
+    lines_y = (block_x, count_y, count_z)
+    deep = min(rows_x, max(1, 32 // (span * 2)))
+    shapes = [
+        straight, (count_x, count_x), (count_y, count_y), (count_z, count_z),
+        turned, (rows_y, count_x, half), (rows_y, 3 * chip_x, half), turned, straight, turned,
+        (rows_y, count_x, half), turned,
+        lines_y, lines_y, lines_y, straight, straight, straight,
+        (chip_x, rows_y, half), (far_block, count_y, half), (far_block, count_y, half),
+        (chip_x, rows_y, half), (rows_y, chip_x, half), (rows_y, chip_x, half),
+        (deep, span, count_z), (num_gy, 8, half), (8, half), (num_gx, 8, half),
+    ]
+    sems = [
+        (4, parts), (6, parts), (3, parts), (2, parts), (4, parts), (6, parts), (3, parts), (2, parts),
+        (4, 2, num_gy), (4, 2, num_gy), (2, num_gy), (2, num_gy), (1,), (1,),
+        (2, num_gx), (2, num_gx), (5,),
+    ]
+    vmem = pl.BlockSpec(memory_space=pltpu.VMEM)
+    potential, partial = pl.pallas_call(
+        functools.partial(chip_kernel, num_gx, num_gy, parts),
+        out_shape=(
+            pltpu.VMEM(straight, jnp.float32),
+            jax.ShapeDtypeStruct((1, 1), jnp.float32),
+        ),
+        in_specs=[pl.BlockSpec(memory_space=pltpu.HBM)] * 4,
+        out_specs=(vmem, vmem),
+        scratch_shapes=[pltpu.VMEM(shape, jnp.float32) for shape in shapes]
+        + [pltpu.SemaphoreType.DMA(shape) for shape in sems],
+        compiler_params=pltpu.CompilerParams(
+            collective_id=0, has_side_effects=True, vmem_limit_bytes=67043328 - 4 * density.size - 2**16
+        ),
+    )(
+        density,
+        jnp.asarray(deriv_matrix(count_x)),
+        jnp.asarray(deriv_matrix(count_y)),
+        jnp.asarray(deriv_matrix(count_z).T.copy()),
+    )
+    return (potential, partial.reshape(()))
 
 
 def body(num_gx, num_gy, density):
@@ -383,5 +967,12 @@
 def solution(mesh):
     in_specs = (P("gx", "gy", None),)
     out_specs = (P("gx", "gy", None), P())
-    run = functools.partial(body, mesh.shape["gx"], mesh.shape["gy"])
+    num_gx, num_gy = mesh.shape["gx"], mesh.shape["gy"]
+
+    def run(density):
+        rows_x, rows_y, count_z = density.shape
+        even = count_z % 256 == 0 and rows_y % 16 == 0 and rows_x % (8 * num_gy) == 0
+        form = chip_body if num_gx == 8 and even else body
+        return form(num_gx, num_gy, density)
+
     return jax.shard_map(run, mesh=mesh, in_specs=in_specs, out_specs=out_specs, check_vma=False)

time: 192 us -> 183 us (0.953); the launches traced: 192 us -> 179 us
  Pallas kernels: 188 us -> 176 us
    pallas_call x1, Pallas kernels: 188 us -> 176 us  [chip_body(): pl.pallas_call(functools.partial(chip_kernel, num_gx, num_gy, parts), out...]
where the time goes in v1:
time: 183 us; the launch traced here: 179 us
  Pallas kernels  176 us (96%)
  between operations  2.33 us (1%)
    pallas_call x1, Pallas kernels, chip_body(): pl.pallas_call(functools.partial(chip_kernel, num_gx, num_gy, parts), out...  176 us

profile of v1, /device:TPU:9, one launch (start us, length us, event | category | flops | bytes accessed | tf_op | source)
XLA Modules:
  0.0 179.2 jit_solution(9555669158399948506)
XLA Ops:
  0.6 175.6 %shard_map.59 = (f32[32,64,256]{2,1,0:T(8,128)S(1)}, f32[1,1]{1,0:T(1,128)}) custom-call(f32[32,64,256]{2,1,0:T(8,128)} %n_hbm.1, f32[256,256]{1,0:T(8,128)} %constant.4.clone.dmx_hbm.dmy_hbm, f32[256,256]{1,0:T(8,128)} %constant.4.clone.dmx_hbm.dmy_hbm, f32[256,256]{1,0:T(8,128)} %constant.5.clone.dmz_hbm), custom_call_target="tpu_custom_call" | custom-call | tf_op jit(solution)/shard_map/pallas_call | solution.py:894
  176.2 1.3 copy.8

commit v2 on v1

--- a/solution.py
+++ b/solution.py
@@ -418,15 +418,30 @@
             barrier, inc=1, device_id={"gy": peer_y(k)}, device_id_type=pl.DeviceIdType.MESH
         )
 
-    def y_copies(phase, c, source, target, forward):
+    y_chunks = (2, 2, parts, 4)
+    y_plan = ((n_ref, ly1), (ry, gy), (gy, ly2), (ry, dy))
+
+    def y_ends(phase, c, to, mine):
+        source, target = y_plan[phase]
+        if phase == 2:
+            line = pl.ds(pl.multiple_of(mine * rows_y + c * span, span), span)
+            return source.at[pl.ds(to * block_x, block_x), ys(c)], target.at[:, line]
+        rows = block_x // y_chunks[phase]
+        if phase == 0:
+            return (
+                source.at[pl.ds(to * block_x + c * rows, rows)],
+                target.at[pl.ds(c * rows, rows), y_rows(mine)],
+            )
+        return (
+            source.at[pl.ds(c * rows, rows), y_rows(to)],
+            target.at[pl.ds(mine * block_x + c * rows, rows)],
+        )
+
+    def y_copies(phase, c):
         copies = []
         for k in far_first(num_gy):
             to = peer_y(k)
-            theirs, mine = pl.ds(to * block_x, block_x), pl.ds(me_y * block_x, block_x)
-            if forward:
-                src, dst = source.at[theirs, :, zs(c)], target.at[:, y_rows(me_y), zs(c)]
-            else:
-                src, dst = source.at[:, y_rows(to), zs(c)], target.at[mine, :, zs(c)]
+            src, dst = y_ends(phase, c, to, me_y)
             copies.append(pltpu.make_async_remote_copy(
                 src_ref=src, dst_ref=dst,
                 send_sem=ys_sem.at[phase, c, k], recv_sem=yr_sem.at[phase, c, k],
@@ -434,71 +449,75 @@
             ))
         return copies
 
-    y_plan = ((n_ref, ly1, True), (ry, gy, False), (gy, ly2, True), (ry, dy, False))
-
     def y_send(phase, c):
-        source, target, forward = y_plan[phase]
-        for copy in y_copies(phase, c, source, target, forward):
+        for copy in y_copies(phase, c):
             copy.start()
-        mine = pl.ds(me_y * block_x, block_x)
-        if forward:
-            target[:, y_rows(me_y), zs(c)] = source[mine, :, zs(c)]
+        here, there = y_ends(phase, c, me_y, me_y)
+        there[...] = here[...]
+
+    def y_wait(phase, sent, chunks=None):
+        for c in range(y_chunks[phase]) if chunks is None else chunks:
+            for copy in y_copies(phase, c):
+                if sent:
+                    copy.wait_send()
+                else:
+                    copy.wait_recv()
+
+    far_chunk = far_block // 2
+
+    def far_copies(phase, h):
+        copies = []
+        for k in far_first(num_gy):
+            to = peer_y(k)
+            if phase == 0:
+                src = far_n.at[pl.ds(to * far_block + h * far_chunk, far_chunk)]
+                dst = far_ly.at[pl.ds(h * far_chunk, far_chunk), y_rows(me_y), :]
+            else:
+                src = far_ry.at[pl.ds(h * far_chunk, far_chunk), y_rows(to), :]
+                dst = far_gy.at[pl.ds(me_y * far_block + h * far_chunk, far_chunk)]
+            copies.append(pltpu.make_async_remote_copy(
+                src_ref=src, dst_ref=dst,
+                send_sem=ws_sem.at[phase, h, k], recv_sem=wr_sem.at[phase, h, k],
+                device_id={"gy": to}, device_id_type=pl.DeviceIdType.MESH,
+            ))
+        return copies
+
+    def far_send(phase, h):
+        for copy in far_copies(phase, h):
+            copy.start()
+        mine = pl.ds(me_y * far_block + h * far_chunk, far_chunk)
+        here = pl.ds(h * far_chunk, far_chunk)
+        if phase == 0:
+            far_ly[here, y_rows(me_y), :] = far_n[mine]
         else:
-            target[mine, :, zs(c)] = source[:, y_rows(me_y), zs(c)]
-
-    def y_wait(phase, c, sent):
-        for copy in y_copies(phase, c, *y_plan[phase]):
+            far_gy[mine] = far_ry[here, y_rows(me_y), :]
+
+    def far_wait(phase, h, sent):
+        for copy in far_copies(phase, h):
             if sent:
                 copy.wait_send()
             else:
                 copy.wait_recv()
 
-    def far_copies(phase):
-        copies = []
-        for k in far_first(num_gy):
-            to = peer_y(k)
-            if phase == 0:
-                src = far_n.at[pl.ds(to * far_block, far_block)]
-                dst = far_ly.at[:, y_rows(me_y), :]
-            else:
-                src = far_ry.at[:, y_rows(to), :]
-                dst = far_gy.at[pl.ds(me_y * far_block, far_block)]
-            copies.append(pltpu.make_async_remote_copy(
-                src_ref=src, dst_ref=dst,
-                send_sem=ws_sem.at[phase, k], recv_sem=wr_sem.at[phase, k],
-                device_id={"gy": to}, device_id_type=pl.DeviceIdType.MESH,
-            ))
-        return copies
-
-    def far_send(phase):
-        for copy in far_copies(phase):
-            copy.start()
-        mine = pl.ds(me_y * far_block, far_block)
-        if phase == 0:
-            far_ly[:, y_rows(me_y), :] = far_n[mine]
-        else:
-            far_gy[mine] = far_ry[:, y_rows(me_y), :]
-
-    def far_wait(phase, sent):
-        for copy in far_copies(phase):
-            if sent:
-                copy.wait_send()
-            else:
-                copy.wait_recv()
+    def halves(values):
+        high = values.astype(jnp.bfloat16)
+        return high, (values - high.astype(jnp.float32)).astype(jnp.bfloat16)
 
     def product(left, right):
-        return jnp.dot(left, right, precision=highest, preferred_element_type=jnp.float32)
-
-    def y_lines(source, c):
-        @pl.loop(0, block_x)
+        (left_high, left_low), (right_high, right_low) = left, right
+        dot = functools.partial(jnp.dot, preferred_element_type=jnp.float32)
+        return dot(left_high, right_high) + (dot(left_high, right_low) + dot(left_low, right_high))
+
+    def y_lines(source, first, last):
+        @pl.loop(first, last)
         def _(i):
-            ry[i, :, zs(c)] = product(dmy_ref[...], source[i, :, zs(c)])
+            ry[i] = product((dmy_ref[0], dmy_ref[1]), halves(source[i]))
 
     group = min(rows_x, max(1, 256 // rows_y))
 
     def along_z(source, i):
         flat = source[pl.ds(i * group, group)].reshape(group * rows_y, count_z)
-        return product(flat, dmz_ref[...]).reshape(group, rows_y, count_z)
+        return product(halves(flat), (dmz_ref[0], dmz_ref[1])).reshape(group, rows_y, count_z)
 
     step = min(8, span)
 
@@ -528,9 +547,20 @@
             ))
         return copies
 
-    def forward_copy(lines, send, recv, s):
-        part = lines.at[ys(s), chip_rows(outer), :]
-        return to_x(opposite * 2 + core, part, part, send.at[3, s], recv.at[5, s])
+    pieces = 2
+
+    def piece(s, u):
+        size = span // pieces
+        return pl.ds(s * span + u * size, size)
+
+    def forward_copies(lines, send, recv, s):
+        copies = []
+        for u in range(pieces):
+            part = lines.at[piece(s, u), chip_rows(outer), :]
+            copies.append(to_x(
+                opposite * 2 + core, part, part, send.at[3 + u, s], recv.at[5 + u, s]
+            ))
+        return copies
 
     def from_outer(lines, recv, s):
         for j in range(2):
@@ -551,33 +581,39 @@
             ))
         return copies
 
-    def back_copies(own, other, target, send, recv, s):
+    def back_copies(own, other, target, send, recv, s, u=None):
+        at = ys(s) if u is None else piece(s, u)
+        slot = s if u is None else s * pieces + u
         copies = []
         for j in range(2):
             copies.append(to_x(
-                outer * 2 + j, g_lines.at[ys(s), local_rows(other + j * rows_x, rows_x), :],
-                target.at[ys(s), :, zs(core)], send.at[j, s], recv.at[core, s],
+                outer * 2 + j, g_lines.at[at, local_rows(other + j * rows_x, rows_x), :],
+                target.at[at, :, zs(core)], send.at[j, slot], recv.at[core, slot],
             ))
         copies.append(to_x(
-            mate, g_lines.at[ys(s), local_rows(own + (1 - core) * rows_x, rows_x), :],
-            target.at[ys(s), :, zs(core)], send.at[2, s], recv.at[core, s],
+            mate, g_lines.at[at, local_rows(own + (1 - core) * rows_x, rows_x), :],
+            target.at[at, :, zs(core)], send.at[2, slot], recv.at[core, slot],
         ))
         return copies
 
     first_own, first_other, first_far = chip_x, jnp.where(low, 0, 2 * chip_x), jnp.where(low, 2 * chip_x, 0)
     second_own, second_other = jnp.where(low, chip_x, 0), jnp.where(low, 0, chip_x)
 
-    def x_back(own, other, target, send, recv, s):
-        for copy in back_copies(own, other, target, send, recv, s):
+    def x_back(own, other, target, send, recv, s, u=None):
+        for copy in back_copies(own, other, target, send, recv, s, u):
             copy.start()
-        target[ys(s), :, zs(core)] = g_lines[ys(s), local_rows(own + core * rows_x, rows_x), :]
-
-    def x_lines(source, first_row, rows, s):
-        @pl.loop(0, span)
+        at = ys(s) if u is None else piece(s, u)
+        target[at, :, zs(core)] = g_lines[at, local_rows(own + core * rows_x, rows_x), :]
+
+    def x_lines(source, first_row, rows, first, count):
+        @pl.loop(0, count // 2)
         def _(j):
-            y = s * span + j
-            matrix = dmx_ref[pl.ds(pl.multiple_of(first_row, chip_x), rows), :]
-            g_lines[y, pl.ds(0, rows), :] = product(matrix, source[y])
+            y = first + 2 * j
+            at = pl.ds(pl.multiple_of(first_row, chip_x), rows)
+            pair = jnp.concatenate([source[y], source[y + 1]], axis=1)
+            result = product((dmx_ref[0, at, :], dmx_ref[1, at, :]), halves(pair))
+            g_lines[y, pl.ds(0, rows), :] = result[:, :half]
+            g_lines[y + 1, pl.ds(0, rows), :] = result[:, half:]
 
     deep = min(rows_x, max(1, 32 // (span * lanes_count)))
 
@@ -608,8 +644,8 @@
         def _(i):
             gz[pl.ds(i * group, group)] = along_z(n_ref, i)
 
-    def z_divergence():
-        @pl.loop(0, rows_x // group)
+    def z_divergence(first=0, last=rows_x // group):
+        @pl.loop(first, last)
         def _(i):
             at = pl.ds(i * group, group)
             out_ref[at] = out_ref[at] - along_z(gz, i)
@@ -651,8 +687,9 @@
         energy_ref[...] = jnp.sum(total, axis=(0, 1), keepdims=True) * (1.0 / cells)
 
     def finish(s, sources):
-        for j in sources:
-            landed(dx_t.at[ys(s), :, zs(j)], dr_sem.at[j, s])
+        for u in range(pieces):
+            for j in sources:
+                landed(dx_t.at[piece(s, u), :, zs(j)], dr_sem.at[j, s * pieces + u])
 
         @pl.loop(0, span // step)
         def _(j):
@@ -670,23 +707,24 @@
                 n_lines[ys(s), x_rows(me_x), :] = n_t[ys(s), :, zs(core)]
 
     def y_first(c):
-        y_wait(0, c, False)
-        y_lines(ly1, c)
+        rows = block_x // 2
+        y_wait(0, False, (c,))
+        y_lines(ly1, c * rows, (c + 1) * rows)
         y_send(1, c)
 
     def y_second(c):
-        y_wait(2, c, False)
+        rows = block_x // 4
         if c == 0:
-            for other in range(lanes_count):
-                y_wait(1, other, True)
-        y_lines(ly2, c)
+            y_wait(2, False)
+            y_wait(1, True)
+        y_lines(ly2, c * rows, (c + 1) * rows)
         y_send(3, c)
 
     acc[...] = jnp.zeros_like(acc)
-    for c in range(lanes_count):
-        loads[c].wait()
-        if c == 0:
-            pl.semaphore_wait(barrier, num_gx + num_gy - 2)
+    for load in loads:
+        load.wait()
+    pl.semaphore_wait(barrier, num_gx + num_gy - 2)
+    for c in range(2):
         y_send(0, c)
 
     def outer_program():
@@ -694,26 +732,23 @@
         for copy in tables:
             copy.wait()
         z_gradient()
-        for c in range(lanes_count):
+        for c in range(2):
             y_first(c)
-        for c in range(lanes_count):
-            y_wait(1, c, False)
+        y_wait(1, False)
         for s in every:
             for j in range(2):
                 landed(gx_t.at[ys(s), :, zs(j)], gr_sem.at[j, s])
             pointwise(s)
             for copy in f_sends(s, "outer"):
                 copy.start()
-        for c in range(lanes_count):
-            y_send(2, c)
+            y_send(2, s)
         energy_first()
         z_divergence()
         energy_second()
-        for c in range(lanes_count):
+        for c in range(4):
             y_second(c)
         energy_last()
-        for c in range(lanes_count):
-            y_wait(3, c, False)
+        y_wait(3, False)
         for s in every:
             finish(s, (0, 1))
         for s in every:
@@ -728,49 +763,68 @@
 
         def pass_on(lines, send, recv, s):
             from_outer(lines, recv, s)
-            forward_copy(lines, send, recv, s).start()
-
-        y_first(0)
-        early = parts // 4
-        for s in range(early):
-            pass_on(n_lines, ns_sem, nr_sem, s)
-        y_first(1)
-        for s in range(early, parts):
-            pass_on(n_lines, ns_sem, nr_sem, s)
+            for copy in forward_copies(lines, send, recv, s):
+                copy.start()
 
         far_rows = chip_rows(opposite)
+        far_group = min(span, max(1, 256 // chip_x))
+
+        def swap(s):
+            return to_x(
+                mate, n_lines.at[ys(s), far_rows, :], far_other.at[ys(s)], os_sem.at[s], or_sem.at[s]
+            )
+
+        def far_z(s):
+            swap(s).wait_recv()
+
+            @pl.loop(0, span // far_group)
+            def _(i):
+                at = pl.ds(s * span + i * far_group, far_group)
+                here = n_lines[at, far_rows, :].reshape(far_group * chip_x, half)
+                there = far_other[at].reshape(far_group * chip_x, half)
+                table = [
+                    jnp.concatenate([dmz_ref[p, zs(core), zs(core)], dmz_ref[p, zs(1 - core), zs(core)]])
+                    for p in range(2)
+                ]
+                result = product(halves(jnp.concatenate([here, there], axis=1)), table)
+                far_gz[at] = result.reshape(far_group, chip_x, half)
+
         for s in every:
             for j in range(2):
                 landed(n_lines.at[ys(s), x_rows(opposite * 2 + j), :], nr_sem.at[2 + j, s])
-        swap = to_x(mate, n_lines.at[:, far_rows, :], far_other, os_sem.at[0], or_sem.at[0])
-        swap.start()
-
-        @pl.loop(0, rows_y // 8)
-        def _(j):
-            y0 = pl.multiple_of(j * 8, 8)
-            far_n[:, pl.ds(y0, 8), :] = jnp.swapaxes(n_lines[pl.ds(y0, 8), far_rows, :], 0, 1)
-
-        far_send(0)
-        swap.wait_recv()
-        far_group = min(rows_y, max(1, 256 // chip_x))
-
-        @pl.loop(0, rows_y // far_group)
-        def _(i):
-            at = pl.ds(i * far_group, far_group)
-            here = n_lines[at, far_rows, :].reshape(far_group * chip_x, half)
-            there = far_other[at].reshape(far_group * chip_x, half)
-            result = product(here, dmz_ref[zs(core), zs(core)])
-            result = result + product(there, dmz_ref[zs(1 - core), zs(core)])
-            far_gz[at] = result.reshape(far_group, chip_x, half)
-
-        def far_lines():
-            far_wait(0, False)
-
-            @pl.loop(0, far_block)
-            def _(i):
-                far_ry[i] = product(dmy_ref[...], far_ly[i])
-
-            far_send(1)
+            swap(s).start()
+
+            @pl.loop(0, span // step)
+            def _(j):
+                y0 = pl.multiple_of(s * span + j * step, step)
+                far_n[:, pl.ds(y0, step), :] = jnp.swapaxes(
+                    n_lines[pl.ds(y0, step), far_rows, :], 0, 1
+                )
+
+            if s == parts - 1:
+                for h in range(2):
+                    far_send(0, h)
+            pass_on(n_lines, ns_sem, nr_sem, s)
+            if s > 0:
+                far_z(s - 1)
+            if s == parts // 4 - 1:
+                y_first(0)
+            if s == parts // 2 - 1:
+                y_first(1)
+        far_z(parts - 1)
+
+        def far_lines(h):
+            far_wait(0, h, False)
+
+            @pl.loop(0, far_chunk // 2)
+            def _(j):
+                i = h * far_chunk + 2 * j
+                pair = jnp.concatenate([far_ly[i], far_ly[i + 1]], axis=1)
+                result = product((dmy_ref[0], dmy_ref[1]), halves(pair))
+                far_ry[i] = result[:, :half]
+                far_ry[i + 1] = result[:, half:]
+
+            far_send(1, h)
 
         def far_pointwise(s):
             @pl.loop(0, span // step)
@@ -797,28 +851,35 @@
                     (d_grad,) = pull(jnp.ones_like(value))
                     f_lines[y, line, :] = 2.0 * d_grad * grad_x
 
-        for c in range(lanes_count):
-            y_wait(1, c, False)
+        y_wait(1, False)
         lag = parts // 2
         for s in every:
-            landed(n_lines.at[ys(s), chip_rows(far_outer), :], nr_sem.at[5, s])
+            for u in range(pieces):
+                landed(n_lines.at[piece(s, u), chip_rows(far_outer), :], nr_sem.at[5 + u, s])
             landed(n_lines.at[ys(s), x_rows(mate), :], nr_sem.at[4, s])
-            x_lines(n_lines, (inner - 1) * chip_x, 3 * chip_x, s)
+            x_lines(n_lines, (inner - 1) * chip_x, 3 * chip_x, s * span, span)
             x_back(first_own, first_other, gx_t, gs_sem, gr_sem, s)
             landed(gx_t.at[ys(s), :, zs(1 - core)], gr_sem.at[1 - core, s])
             pointwise(s)
             for copy in f_sends(s, "inner"):
                 copy.start()
             f_lines[ys(s), x_rows(me_x), :] = fx_t[ys(s), :, zs(core)]
-            if s == lag:
-                far_lines()
+            if s == parts // 4 - 1:
+                far_lines(0)
+            if s == parts // 2 - 1:
+                far_lines(1)
+                for ready in range(s):
+                    y_send(2, ready)
+            if s >= parts // 2 - 1:
+                y_send(2, s)
             if s >= lag:
                 pass_on(f_lines, fs_sem, fr_sem, s - lag)
-        for c in range(lanes_count):
-            y_send(2, c)
         energy_first()
-        swap.wait_send()
-        far_wait(1, False)
+        for s in every:
+            swap(s).wait_send()
+        for h in range(2):
+            far_wait(1, h, False)
+        slices = rows_x // group
         for s in every:
             far_pointwise(s)
             if s < parts - lag:
@@ -826,40 +887,51 @@
             for copy in back_copies(first_own, first_other, gx_t, gs_sem, gr_sem, s):
                 copy.wait_send()
             landed(f_lines.at[ys(s), x_rows(mate), :], fr_sem.at[4, s])
-            landed(f_lines.at[ys(s), chip_rows(far_outer), :], fr_sem.at[5, s])
-            x_lines(f_lines, (inner - 1) * 2 * chip_x, 2 * chip_x, s)
-            x_back(second_own, second_other, dx_t, ds_sem, dr_sem, s)
-            if s == parts // 4:
-                y_second(0)
-            if s == parts // 2:
-                y_second(1)
+            for u in range(pieces):
+                landed(f_lines.at[piece(s, u), chip_rows(far_outer), :], fr_sem.at[5 + u, s])
+                size = span // pieces
+                x_lines(
+                    f_lines, (inner - 1) * 2 * chip_x, 2 * chip_x, s * span + u * size, size
+                )
+                x_back(second_own, second_other, dx_t, ds_sem, dr_sem, s, u)
+            z_divergence(s * slices // parts, (s + 1) * slices // parts)
+            if s in (parts // 4, parts // 4 + 1):
+                y_second(2 * (s - parts // 4))
+                y_second(2 * (s - parts // 4) + 1)
             if s == parts // 2 + 1:
                 energy_second()
-        z_divergence()
         energy_last()
-        for c in range(lanes_count):
-            y_wait(3, c, False)
+        y_wait(3, False)
         for s in every:
             finish(s, (1 - core,))
         for s in every:
             for copy in n_sends(s, "inner") + f_sends(s, "inner"):
                 copy.wait_send()
-            forward_copy(n_lines, ns_sem, nr_sem, s).wait_send()
-            forward_copy(f_lines, fs_sem, fr_sem, s).wait_send()
-            for copy in back_copies(second_own, second_other, dx_t, ds_sem, dr_sem, s):
+            for copy in forward_copies(n_lines, ns_sem, nr_sem, s):
                 copy.wait_send()
+            for copy in forward_copies(f_lines, fs_sem, fr_sem, s):
+                copy.wait_send()
+            for u in range(pieces):
+                for copy in back_copies(second_own, second_other, dx_t, ds_sem, dr_sem, s, u):
+                    copy.wait_send()
         for phase in range(2):
-            far_wait(phase, True)
+            for h in range(2):
+                far_wait(phase, h, True)
 
     pl.when(is_inner)(inner_program)
     pl.when(jnp.logical_not(is_inner))(outer_program)
 
-    for c in range(lanes_count):
-        for phase in (0, 2, 3):
-            y_wait(phase, c, True)
+    for phase in (0, 2, 3):
+        y_wait(phase, True)
     for phase in range(2):
         for copy in energy_copies(phase):
             copy.wait_send()
+
+
+def two_parts(matrix):
+    high = matrix.astype(jnp.bfloat16)
+    low = (matrix - high.astype(np.float32)).astype(jnp.bfloat16)
+    return jnp.asarray(np.stack([high, low]))
 
 
 def chip_body(num_gx, num_gy, density):
@@ -877,7 +949,6 @@
     lines_y = (block_x, count_y, count_z)
     deep = min(rows_x, max(1, 32 // (span * 2)))
     shapes = [
-        straight, (count_x, count_x), (count_y, count_y), (count_z, count_z),
         turned, (rows_y, count_x, half), (rows_y, 3 * chip_x, half), turned, straight, turned,
         (rows_y, count_x, half), turned,
         lines_y, lines_y, lines_y, straight, straight, straight,
@@ -886,8 +957,9 @@
         (deep, span, count_z), (num_gy, 8, half), (8, half), (num_gx, 8, half),
     ]
     sems = [
-        (4, parts), (6, parts), (3, parts), (2, parts), (4, parts), (6, parts), (3, parts), (2, parts),
-        (4, 2, num_gy), (4, 2, num_gy), (2, num_gy), (2, num_gy), (1,), (1,),
+        (5, parts), (7, parts), (3, parts), (2, parts),
+        (5, parts), (7, parts), (3, 2 * parts), (2, 2 * parts),
+        (4, parts, num_gy), (4, parts, num_gy), (2, 2, num_gy), (2, 2, num_gy), (parts,), (parts,),
         (2, num_gx), (2, num_gx), (5,),
     ]
     vmem = pl.BlockSpec(memory_space=pltpu.VMEM)
@@ -899,16 +971,18 @@
         ),
         in_specs=[pl.BlockSpec(memory_space=pltpu.HBM)] * 4,
         out_specs=(vmem, vmem),
-        scratch_shapes=[pltpu.VMEM(shape, jnp.float32) for shape in shapes]
+        scratch_shapes=[pltpu.VMEM(straight, jnp.float32)]
+        + [pltpu.VMEM((2, count, count), jnp.bfloat16) for count in (count_x, count_y, count_z)]
+        + [pltpu.VMEM(shape, jnp.float32) for shape in shapes]
         + [pltpu.SemaphoreType.DMA(shape) for shape in sems],
         compiler_params=pltpu.CompilerParams(
             collective_id=0, has_side_effects=True, vmem_limit_bytes=67043328 - 4 * density.size - 2**16
         ),
     )(
         density,
-        jnp.asarray(deriv_matrix(count_x)),
-        jnp.asarray(deriv_matrix(count_y)),
-        jnp.asarray(deriv_matrix(count_z).T.copy()),
+        two_parts(deriv_matrix(count_x)),
+        two_parts(deriv_matrix(count_y)),
+        two_parts(deriv_matrix(count_z).T.copy()),
     )
     return (potential, partial.reshape(()))
 
@@ -971,7 +1045,7 @@
 
     def run(density):
         rows_x, rows_y, count_z = density.shape
-        even = count_z % 256 == 0 and rows_y % 16 == 0 and rows_x % (8 * num_gy) == 0
+        even = count_z % 256 == 0 and rows_y % 32 == 0 and rows_x % (8 * num_gy) == 0
         form = chip_body if num_gx == 8 and even else body
         return form(num_gx, num_gy, density)
 

time: 183 us -> 162 us (0.89)
  Pallas kernels: 176 us -> 156 us
    pallas_call x1, Pallas kernels: 176 us -> 156 us  [chip_body(): pl.pallas_call(functools.partial(chip_kernel, num_gx, num_gy, parts), out...]
where the time goes in v2:
time: 162 us; the launch traced here: 159 us
  Pallas kernels  156 us (96%)
  between operations  2.33 us (1%)
    pallas_call x1, Pallas kernels, chip_body(): pl.pallas_call(functools.partial(chip_kernel, num_gx, num_gy, parts), out...  156 us

profile of v2, /device:TPU:9, one launch (start us, length us, event | category | flops | bytes accessed | tf_op | source)
XLA Modules:
  0.0 159.3 jit_solution(17404884809433134715)
XLA Ops:
  0.6 155.6 %shard_map.59 = (f32[32,64,256]{2,1,0:T(8,128)S(1)}, f32[1,1]{1,0:T(1,128)}) custom-call(f32[32,64,256]{2,1,0:T(8,128)} %n_hbm.1, bf16[2,256,256]{2,1,0:T(8,128)(2,1)} %constant.4.clone.dmx_hbm.dmy_hbm, bf16[2,256,256]{2,1,0:T(8,128)(2,1)} %constant.4.clone.dmx_hbm.dmy_hbm, bf16[2,256,256]{2,1,0:T(8,128)(2,1)} %constant.5.clone.dmz_hbm), custom_call_target="tpu_custom_call" | custom-call | tf_op jit(solution)/shard_map/pallas_call | solution.py:966
  156.3 1.3 copy.8

commit v3 on v2

--- a/solution.py
+++ b/solution.py
@@ -743,10 +743,10 @@
                 copy.start()
             y_send(2, s)
         energy_first()
-        z_divergence()
-        energy_second()
         for c in range(4):
             y_second(c)
+        energy_second()
+        z_divergence()
         energy_last()
         y_wait(3, False)
         for s in every:
@@ -853,12 +853,36 @@
 
         y_wait(1, False)
         lag = parts // 2
+        slices = rows_x // group
+
+        def far_step(s):
+            far_pointwise(s)
+            if s < parts - lag:
+                pass_on(f_lines, fs_sem, fr_sem, lag + s)
+            for copy in back_copies(first_own, first_other, gx_t, gs_sem, gr_sem, s):
+                copy.wait_send()
+            landed(f_lines.at[ys(s), x_rows(mate), :], fr_sem.at[4, s])
+            for u in range(pieces):
+                landed(f_lines.at[piece(s, u), chip_rows(far_outer), :], fr_sem.at[5 + u, s])
+                size = span // pieces
+                x_lines(
+                    f_lines, (inner - 1) * 2 * chip_x, 2 * chip_x, s * span + u * size, size
+                )
+                x_back(second_own, second_other, dx_t, ds_sem, dr_sem, s, u)
+
         for s in every:
+            landed(n_lines.at[ys(s), x_rows(mate), :], nr_sem.at[4, s])
             for u in range(pieces):
                 landed(n_lines.at[piece(s, u), chip_rows(far_outer), :], nr_sem.at[5 + u, s])
-            landed(n_lines.at[ys(s), x_rows(mate), :], nr_sem.at[4, s])
             x_lines(n_lines, (inner - 1) * chip_x, 3 * chip_x, s * span, span)
             x_back(first_own, first_other, gx_t, gs_sem, gr_sem, s)
+            if s == parts - 1:
+                pass_on(f_lines, fs_sem, fr_sem, s - lag)
+                for other in every:
+                    swap(other).wait_send()
+                for h in range(2):
+                    far_wait(1, h, False)
+                far_step(0)
             landed(gx_t.at[ys(s), :, zs(1 - core)], gr_sem.at[1 - core, s])
             pointwise(s)
             for copy in f_sends(s, "inner"):
@@ -872,28 +896,12 @@
                     y_send(2, ready)
             if s >= parts // 2 - 1:
                 y_send(2, s)
-            if s >= lag:
+            if lag <= s < parts - 1:
                 pass_on(f_lines, fs_sem, fr_sem, s - lag)
         energy_first()
         for s in every:
-            swap(s).wait_send()
-        for h in range(2):
-            far_wait(1, h, False)
-        slices = rows_x // group
-        for s in every:
-            far_pointwise(s)
-            if s < parts - lag:
-                pass_on(f_lines, fs_sem, fr_sem, lag + s)
-            for copy in back_copies(first_own, first_other, gx_t, gs_sem, gr_sem, s):
-                copy.wait_send()
-            landed(f_lines.at[ys(s), x_rows(mate), :], fr_sem.at[4, s])
-            for u in range(pieces):
-                landed(f_lines.at[piece(s, u), chip_rows(far_outer), :], fr_sem.at[5 + u, s])
-                size = span // pieces
-                x_lines(
-                    f_lines, (inner - 1) * 2 * chip_x, 2 * chip_x, s * span + u * size, size
-                )
-                x_back(second_own, second_other, dx_t, ds_sem, dr_sem, s, u)
+            if s > 0:
+                far_step(s)
             z_divergence(s * slices // parts, (s + 1) * slices // parts)
             if s in (parts // 4, parts // 4 + 1):
                 y_second(2 * (s - parts // 4))

time: 162 us -> 162 us (level)
  no operation moved by 1% of the time
where the time goes in v3:
time: 162 us; the launch traced here: 159 us
  Pallas kernels  156 us (96%)
  between operations  2.33 us (1%)
    pallas_call x1, Pallas kernels, chip_body(): pl.pallas_call(functools.partial(chip_kernel, num_gx, num_gy, parts), out...  156 us

profile of v3, /device:TPU:9, one launch (start us, length us, event | category | flops | bytes accessed | tf_op | source)
XLA Modules:
  0.0 159.3 jit_solution(8757409821744079233)
XLA Ops:
  0.6 155.6 %shard_map.59 = (f32[32,64,256]{2,1,0:T(8,128)S(1)}, f32[1,1]{1,0:T(1,128)}) custom-call(f32[32,64,256]{2,1,0:T(8,128)} %n_hbm.1, bf16[2,256,256]{2,1,0:T(8,128)(2,1)} %constant.4.clone.dmx_hbm.dmy_hbm, bf16[2,256,256]{2,1,0:T(8,128)(2,1)} %constant.4.clone.dmx_hbm.dmy_hbm, bf16[2,256,256]{2,1,0:T(8,128)(2,1)} %constant.5.clone.dmz_hbm), custom_call_target="tpu_custom_call" | custom-call | tf_op jit(solution)/shard_map/pallas_call | solution.py:974
  156.3 1.3 copy.8
